TPU v7x, 32 devices: a whole 2x2x4 slice. The times are simulated.
32 devices in a mesh: lat: 8 (over z, x), lev: 4 (over y, core).
Axes of the slice: x: 2, y: 2, z: 4, core: 2. Of those that a mesh axis runs over, the one named last changes fastest.
Arguments:
- right_side: float32 [8, 64, 2048], P('lev', 'lat'), may hold values from -6 to 6
- diag_shift: float32 [8, 64, 2048], P('lev', 'lat'), may hold values from 0.5 to 2
- level_scale: float32 [8], P('lev'), may hold values from 0.1 to 1
Outputs:
- solution: float32 [8, 64, 2048], P('lev', 'lat')
- residual: float32 [8, 64, 2048], P('lev', 'lat')
All inputs are finite; a program needn't handle non-finite values.
Results may differ from a plain program's by a relative error of at most 0.0003.
Values sent between devices are 32-bit elements; how exact they have to be, the bound alone decides.
A program may use at most 64 MiB of HBM per device.

v0:
```python
import jax
import jax.numpy as jnp
from jax import lax
from jax.sharding import PartitionSpec as P

WAVES = 640
ITERS = 3


def with_halo(block, sides, width):
    for axis, dim in sides:
        count = lax.axis_size(axis)
        forward = [(i, i + 1) for i in range(count - 1)]
        backward = [(target, source) for source, target in forward]
        low = lax.ppermute(
            lax.slice_in_dim(block, block.shape[dim] - width, None, axis=dim), axis, forward
        )
        high = lax.ppermute(lax.slice_in_dim(block, 0, width, axis=dim), axis, backward)
        block = jnp.concatenate([low, block, high], axis=dim)
    return block


def polar_gain(total_rows, start, count):
    latitude = (start + jnp.arange(count, dtype=jnp.int32)).astype(jnp.float32)
    colatitude = jnp.pi * (4.0 * latitude + 3.0) / (4.0 * total_rows + 2.0)
    return 1.0 / jnp.maximum(jnp.sin(colatitude), 0.5) ** 2


def fourier_table(longitudes, wavenumber, cosine_part):
    position = jnp.arange(longitudes, dtype=jnp.int32)
    product = position[:, None] * wavenumber[None, :] % longitudes
    radians = 2.0 * jnp.pi / longitudes * product.astype(jnp.float32)
    return jnp.where(cosine_part[None, :], jnp.cos(radians), jnp.sin(radians))


def sine_table(latitudes):
    counter = jnp.arange(1, latitudes + 1, dtype=jnp.int32)
    product = counter[:, None] * counter[None, :] % (2 * latitudes + 2)
    return jnp.sin(jnp.pi / (latitudes + 1) * product.astype(jnp.float32))


def spectral_weights(latitudes, longitudes, wavenumber):
    counter = jnp.arange(1, latitudes + 1, dtype=jnp.int32).astype(jnp.float32)
    zonal_part = 4.0 * jnp.sin(jnp.pi / longitudes * wavenumber.astype(jnp.float32)) ** 2
    merid_part = 4.0 * jnp.sin(0.5 * jnp.pi / (latitudes + 1) * counter) ** 2
    scaling = 2.0 / (longitudes * (latitudes + 1))
    return scaling / (1.0 + merid_part[:, None] + zonal_part[None, :])


def stencil(padded, diagonal, level_scale, zonal_gain):
    centre = padded[:, 1:-1, :]
    meridional = padded[:, :-2, :] + padded[:, 2:, :]
    zonal_pair = jnp.roll(centre, 1, axis=2) + jnp.roll(centre, -1, axis=2)
    corners = jnp.roll(meridional, 1, axis=2) + jnp.roll(meridional, -1, axis=2)
    coupling = zonal_gain[None, :, None] * zonal_pair + meridional + 0.125 * corners
    return diagonal * centre - level_scale[:, None, None] * coupling


def operate(field, diagonal, level_scale, zonal_gain):
    padded = with_halo(field, (("lat", 1),), 1)
    midway = field.shape[2] // 2
    position = lax.axis_index("lat")
    final_band = lax.axis_size("lat") - 1
    northern = jnp.roll(field[:, :1, :], midway, axis=2)
    southern = jnp.roll(field[:, -1:, :], midway, axis=2)
    upper_row = jnp.where(position == 0, northern, padded[:, :1, :])
    lower_row = jnp.where(position == final_band, southern, padded[:, -1:, :])
    padded = jnp.concatenate([upper_row, padded[:, 1:-1, :], lower_row], axis=1)
    return stencil(padded, diagonal, level_scale, zonal_gain)


def precondition(current, diagonal, fourier, sines, spectral):
    highest = lax.Precision.HIGHEST
    levels, band_rows, longitudes = current.shape
    columns = fourier.shape[1]
    flattened = current.reshape(levels * band_rows, longitudes)
    coefficients = jnp.dot(
        flattened, fourier, precision=highest, preferred_element_type=jnp.float32
    )
    coefficients = coefficients.reshape(levels, band_rows, columns)

    def meridional(received):
        modes = jnp.einsum("kjc,jl->klc", received, sines, precision=highest) * spectral[None]
        returned = jnp.einsum("klc,jl->kjc", modes, sines, precision=highest)
        return lax.all_to_all(returned, "lat", split_axis=1, concat_axis=2, tiled=True)

    arrived = meridional(
        lax.all_to_all(coefficients, "lat", split_axis=2, concat_axis=1, tiled=True)
    )
    synthesis = lax.dot_general(
        arrived.reshape(levels * band_rows, columns),
        fourier,
        (((1,), (1,)), ((), ())),
        precision=highest,
        preferred_element_type=jnp.float32,
    )
    return 0.5 * current / diagonal + synthesis.reshape(levels, band_rows, longitudes)


def paired_products(residual, adjusted, applied):
    return lax.psum((jnp.sum(residual * adjusted), jnp.sum(applied * adjusted)), ("lat", "lev"))


def body(right_side, diag_shift, level_scale):
    levels, band_rows, longitudes = right_side.shape
    bands = lax.axis_size("lat")
    latitudes = band_rows * bands
    position = lax.axis_index("lat")
    zonal_gain = polar_gain(latitudes, position * band_rows, band_rows)
    diagonal = diag_shift + level_scale[:, None, None] * (2.0 * zonal_gain[None, :, None] + 2.5)
    per_device = WAVES // bands
    columns = jnp.arange(2 * WAVES, dtype=jnp.int32)
    remainder = columns % (2 * per_device)
    wavenumber = columns // (2 * per_device) * per_device + remainder % per_device
    fourier = fourier_table(longitudes, wavenumber, remainder < per_device)
    sines = sine_table(latitudes)
    local_columns = jnp.arange(2 * per_device, dtype=jnp.int32)
    local_waves = position * per_device + local_columns % per_device
    spectral = spectral_weights(latitudes, longitudes, local_waves)

    def apply_operator(field):
        return operate(field, diagonal, level_scale, zonal_gain)

    def apply_inverse(current):
        return precondition(current, diagonal, fourier, sines, spectral)

    solution = jnp.zeros_like(right_side)
    residual = right_side
    adjusted = apply_inverse(residual)
    applied = apply_operator(adjusted)
    aligned, curvature = paired_products(residual, adjusted, applied)
    step_size = aligned / curvature
    direction, image = (adjusted, applied)
    for iteration in range(ITERS):
        solution = solution + step_size * direction
        residual = residual - step_size * image
        if iteration + 1 < ITERS:
            adjusted = apply_inverse(residual)
            applied = apply_operator(adjusted)
            aligned_next, curvature = paired_products(residual, adjusted, applied)
            beta_ratio = aligned_next / aligned
            step_size = aligned_next / (curvature - beta_ratio * aligned_next / step_size)
            direction = adjusted + beta_ratio * direction
            image = applied + beta_ratio * image
            aligned = aligned_next
    return (solution, residual)


def solution(mesh):
    placed = (P("lev", "lat", None), P("lev", "lat", None), P("lev"))
    return jax.shard_map(
        body,
        mesh=mesh,
        in_specs=placed,
        out_specs=(P("lev", "lat", None), P("lev", "lat", None)),
        check_vma=False,
    )
```

profile of v0, /device:TPU:0, one launch (start us, length us, event | category | flops | bytes accessed | tf_op | source)
XLA Modules:
  0.0 550.7 jit_solution(15155512000663679863)
XLA Ops:
  0.7 47.8 %fusion.17 = f32[2,8,1280]{2,1,0:T(8,128)S(1)} fusion(s32[1280]{0:T(1024)S(1)} %fusion.99, pred[1280]{0:T(1024)(128)(4,1)S(1)} %fusion.104, f32[2,8,2048]{2,1,0:T(8,128)} %param.3), kind=kOutput, calls=%fused_computation.21 | convolution fusion | flops 542638080 | bytes 219392 | tf_op jit(solution)/shard_map/dot_general | solution.py:77
  48.5 0.6 copy.36
  49.1 2.8 reshape.181
  51.9 7.6 %all-to-all-start = ((f32[8,1,2560]{2,1,0:T(1,128)}), f32[8,1,2560]{2,1,0:T(1,128)S(1)}, u32[]{:S(2)}, u32[]{:S(2)}) async-start(f32[8,1,2560]{2,1,0:T(1,128)} %reshape.181), calls=%async_computation | async-start | bytes 163840 | tf_op jit(solution)/shard_map/all_to_all | solution.py:88
  59.7 6.7 %all-to-all-done = f32[8,1,2560]{2,1,0:T(1,128)S(1)} async-done(((f32[8,1,2560]{2,1,0:T(1,128)}), f32[8,1,2560]{2,1,0:T(1,128)S(1)}, u32[]{:S(2)}, u32[]{:S(2)}) %all-to-all-start) | async-done | bytes 81952 | tf_op jit(solution)/shard_map/all_to_all | solution.py:88
  66.9 0.8 reduce
  67.8 2.0 reshape.182
  69.8 0.7 copy.59
  71.5 0.8 copy.40
  72.3 3.4 all-to-all-start.1
  75.8 7.1 %all-to-all-done.1 = f32[2,64,160]{2,0,1:T(2,128)S(1)} async-done(((f32[2,64,160]{2,0,1:T(2,128)}), f32[2,64,160]{2,0,1:T(2,128)S(1)}, u32[]{:S(2)}, u32[]{:S(2)}) %all-to-all-start.1) | async-done | bytes 81952 | tf_op jit(solution)/shard_map/all_to_all | solution.py:85
  83.1 50.1 %fusion.18 = f32[2,8,2048]{2,1,0:T(8,128)S(1)} fusion(f32[2,8,1280]{2,1,0:T(8,128)S(1)} %dot_general.48, s32[1280]{0:T(1024)S(1)} %fusion.99, pred[1280]{0:T(1024)(128)(4,1)S(1)} %fusion.104, f32[2,8,2048]{2,1,0:T(8,128)S(1)} %copy-done.1, f32[2,8,2048]{2,1,0:T(8,128)S(1)} %copy-done, f32[2,8]{1,0:T(2,128)S(1)} %broadcast_multiply_fusion), kind=kOutput, calls=%fused_computation.22 | convolution fusion | flops 542769152 | bytes 481600 | tf_op jit(solution)/shard_map/dot_general | solution.py:90
  133.4 2.1 collective-permute-start
  135.6 1.3 collective-permute-start.1
  136.9 4.2 collective-permute-done.1
  141.4 0.8 multiply_reduce_fusion.4
  142.2 49.2 %all-reduce.2 = (f32[]{:T(128)}, f32[]{:T(128)}) all-reduce(f32[]{:T(128)} %get-tuple-element.7, f32[]{:T(128)} %get-tuple-element.6), channel_id=1, replica_groups=mesh['lat'=8,'lev'=4] {'lat','lev'}, use_global_device_ids=true, to_apply=%region_1.2 | all-reduce | flops 2 | bytes 16 | tf_op jit(solution)/shard_map/psum | solution.py:101
  192.8 46.1 %fusion.9 = f32[2,8,1280]{2,1,0:T(8,128)S(1)} fusion(f32[2,8,2048]{2,1,0:T(8,128)S(1)} %multiply_subtract_fusion.2, s32[1280]{0:T(1024)S(1)} %fusion.99, pred[1280]{0:T(1024)(128)(4,1)S(1)} %fusion.104), kind=kOutput, calls=%fused_computation.12 | convolution fusion | flops 542638080 | bytes 219392 | tf_op jit(solution)/shard_map/dot_general | solution.py:77
  238.9 0.6 copy.42
  239.6 2.1 reshape.183
  241.7 11.4 %all_to_all.99 = f32[8,1,2560]{2,1,0:T(1,128)S(1)} all-to-all(f32[8,1,2560]{2,1,0:T(1,128)S(1)} %reshape.183), channel_id=1, replica_groups=mesh['lat'=8,'lev'=4] {'lat'}, dimensions={0} | all-to-all | bytes 163840 | tf_op jit(solution)/shard_map/all_to_all | solution.py:88
  253.1 0.8 reduce.1
  254.0 2.0 reshape.184
  256.0 0.7 copy.62
  256.7 0.5 fusion.28
  257.8 9.7 %all_to_all.100 = f32[2,64,160]{2,0,1:T(2,128)S(1)} all-to-all(f32[2,64,160]{2,0,1:T(2,128)S(1)} %copy.46), channel_id=1, replica_groups=mesh['lat'=8,'lev'=4] {'lat'}, dimensions={1} | all-to-all | bytes 163840 | tf_op jit(solution)/shard_map/all_to_all | solution.py:85
  267.7 50.1 %fusion.21 = f32[2,8,2048]{2,1,0:T(8,128)S(1)} fusion(f32[2,8,1280]{2,1,0:T(8,128)S(1)} %dot_general.53, s32[1280]{0:T(1024)S(1)} %fusion.99, pred[1280]{0:T(1024)(128)(4,1)S(1)} %fusion.104, f32[2,8,2048]{2,1,0:T(8,128)S(1)} %multiply_subtract_fusion.2, f32[2,8,2048]{2,1,0:T(8,128)S(1)} %copy-done, f32[2,8]{1,0:T(2,128)S(1)} %broadcast_multiply_fusion), kind=kOutput, calls=%fused_computation.23 | convolution fusion | flops 542769152 | bytes 481600 | tf_op jit(solution)/shard_map/dot_general | solution.py:90
  317.9 2.1 collective-permute-start.2
  320.1 1.3 collective-permute-start.3
  321.5 4.2 collective-permute-done.3
  326.0 0.9 multiply_reduce_fusion.2
  326.9 40.1 %all-reduce.1 = (f32[]{:T(128)}, f32[]{:T(128)}) all-reduce(f32[]{:T(128)} %get-tuple-element.5, f32[]{:T(128)} %get-tuple-element.4), channel_id=1, replica_groups=mesh['lat'=8,'lev'=4] {'lat','lev'}, use_global_device_ids=true, to_apply=%region_5.6 | all-reduce | flops 2 | bytes 16 | tf_op jit(solution)/shard_map/psum | solution.py:101
  371.4 46.1 %fusion.5 = f32[2,8,1280]{2,1,0:T(8,128)S(1)} fusion(f32[2,8,2048]{2,1,0:T(8,128)S(1)} %multiply_subtract_fusion.1, s32[1280]{0:T(1024)S(1)} %fusion.99, pred[1280]{0:T(1024)(128)(4,1)S(1)} %fusion.104), kind=kOutput, calls=%fused_computation.8 | convolution fusion | flops 542638080 | bytes 219392 | tf_op jit(solution)/shard_map/dot_general | solution.py:77
  417.5 0.6 copy.48
  418.2 2.1 reshape.185
  420.3 11.4 %all_to_all.101 = f32[8,1,2560]{2,1,0:T(1,128)S(1)} all-to-all(f32[8,1,2560]{2,1,0:T(1,128)S(1)} %reshape.185), channel_id=1, replica_groups=mesh['lat'=8,'lev'=4] {'lat'}, dimensions={0} | all-to-all | bytes 163840 | tf_op jit(solution)/shard_map/all_to_all | solution.py:88
  431.7 0.8 reduce.2
  432.6 2.0 reshape.186
  434.6 0.7 copy.65
  435.3 0.5 fusion.27
  436.4 9.7 %all_to_all.102 = f32[2,64,160]{2,0,1:T(2,128)S(1)} all-to-all(f32[2,64,160]{2,0,1:T(2,128)S(1)} %copy.52), channel_id=1, replica_groups=mesh['lat'=8,'lev'=4] {'lat'}, dimensions={1} | all-to-all | bytes 163840 | tf_op jit(solution)/shard_map/all_to_all | solution.py:85
  446.3 50.1 %fusion.24 = f32[2,8,2048]{2,1,0:T(8,128)S(1)} fusion(f32[2,8,1280]{2,1,0:T(8,128)S(1)} %dot_general.58, s32[1280]{0:T(1024)S(1)} %fusion.99, pred[1280]{0:T(1024)(128)(4,1)S(1)} %fusion.104, f32[2,8,2048]{2,1,0:T(8,128)S(1)} %multiply_subtract_fusion.1, f32[2,8,2048]{2,1,0:T(8,128)S(1)} %copy-done, f32[2,8]{1,0:T(2,128)S(1)} %broadcast_multiply_fusion), kind=kOutput, calls=%fused_computation.24 | convolution fusion | flops 542769152 | bytes 481600 | tf_op jit(solution)/shard_map/dot_general | solution.py:90
  496.5 2.1 collective-permute-start.4
  498.7 1.3 collective-permute-start.5
  500.1 4.2 collective-permute-done.5
  504.6 0.8 multiply_reduce_fusion
  505.4 40.3 %all-reduce = (f32[]{:T(128)}, f32[]{:T(128)}) all-reduce(f32[]{:T(128)} %get-tuple-element.3, f32[]{:T(128)} %get-tuple-element.2), channel_id=1, replica_groups=mesh['lat'=8,'lev'=4] {'lat','lev'}, use_global_device_ids=true, to_apply=%region_9.10 | all-reduce | flops 2 | bytes 16 | tf_op jit(solution)/shard_map/psum | solution.py:101
  549.6 0.8 multiply_subtract_fusion
  (60 shorter events, 5.2 us)
Async XLA Ops:
  51.9 14.5 %all-to-all-start = ((f32[8,1,2560]{2,1,0:T(1,128)}), f32[8,1,2560]{2,1,0:T(1,128)S(1)}, u32[]{:S(2)}, u32[]{:S(2)}) async-start(f32[8,1,2560]{2,1,0:T(1,128)} %reshape.181), calls=%async_computation | async-start | bytes 163840 | tf_op jit(solution)/shard_map/all_to_all | solution.py:88
  69.8 5.9 %copy-start.2 = (f32[2]{0:T(128)S(1)}, f32[2]{0:T(128)}, u32[]{:S(2)}) copy-start(f32[2]{0:T(128)} %param.5) | copy-start | bytes 28
  69.8 13.3 %copy-start = (f32[2,8,2048]{2,1,0:T(8,128)S(1)}, f32[2,8,2048]{2,1,0:T(8,128)}, u32[]{:S(2)}) copy-start(f32[2,8,2048]{2,1,0:T(8,128)} %param.4) | copy-start | bytes 393220
  69.8 13.3 %copy-start.1 = (f32[2,8,2048]{2,1,0:T(8,128)S(1)}, f32[2,8,2048]{2,1,0:T(8,128)}, u32[]{:S(2)}) copy-start(f32[2,8,2048]{2,1,0:T(8,128)} %param.3) | copy-start | bytes 393220
  72.3 10.7 %all-to-all-start.1 = ((f32[2,64,160]{2,0,1:T(2,128)}), f32[2,64,160]{2,0,1:T(2,128)S(1)}, u32[]{:S(2)}, u32[]{:S(2)}) async-start(f32[2,64,160]{2,0,1:T(2,128)} %copy.40), calls=%async_computation.1 | async-start | bytes 262144 | tf_op jit(solution)/shard_map/all_to_all | solution.py:85
  133.4 3.6 collective-permute-start
  135.6 5.6 %collective-permute-start.1 = (f32[2,1,2048]{2,1,0:T(1,128)S(1)}, f32[2,1,2048]{2,1,0:T(1,128)S(1)}, u32[]{:S(2)}, u32[]{:S(2)}) collective-permute-start(f32[2,1,2048]{2,1,0:T(1,128)S(1)} %get-tuple-element.58), channel_id=1, source_target_pairs={{4,0},{8,4},{12,8},{16,12},{20,16},{24,20},{28,24},{5,1},{9,5},{13... | collective-permute-start | bytes 49160 | tf_op jit(solution)/shard_map/ppermute | solution.py:18
  317.9 3.6 collective-permute-start.2
  320.1 5.6 %collective-permute-start.3 = (f32[2,1,2048]{2,1,0:T(1,128)S(1)}, f32[2,1,2048]{2,1,0:T(1,128)S(1)}, u32[]{:S(2)}, u32[]{:S(2)}) collective-permute-start(f32[2,1,2048]{2,1,0:T(1,128)S(1)} %get-tuple-element.44), channel_id=1, source_target_pairs={{4,0},{8,4},{12,8},{16,12},{20,16},{24,20},{28,24},{5,1},{9,5},{13... | collective-permute-start | bytes 49160 | tf_op jit(solution)/shard_map/ppermute | solution.py:18
  496.5 3.6 collective-permute-start.4
  498.7 5.6 %collective-permute-start.5 = (f32[2,1,2048]{2,1,0:T(1,128)S(1)}, f32[2,1,2048]{2,1,0:T(1,128)S(1)}, u32[]{:S(2)}, u32[]{:S(2)}) collective-permute-start(f32[2,1,2048]{2,1,0:T(1,128)S(1)} %get-tuple-element.30), channel_id=1, source_target_pairs={{4,0},{8,4},{12,8},{16,12},{20,16},{24,20},{28,24},{5,1},{9,5},{13... | collective-permute-start | bytes 49160 | tf_op jit(solution)/shard_map/ppermute | solution.py:18
where the time goes:
time: 560 us; the launch traced here: 551 us
  matrix products  293 us (52%)
  blocking collectives  172 us (31%)
  waiting for transfers between devices  26.8 us (5%)
  starting transfers between devices  21.1 us (4%)
  local copies, waits for them, and re-layouts  20.1 us (4%)
  between operations  11.2 us (2%)
  other arithmetic  6.44 us (1%)
    dot_general x3, matrix products, precondition(): lax.dot_general(arrived.reshape(levels * band_rows, columns), fourier, ((...  150 us
    dot_general x3, matrix products, precondition(): jnp.dot(flattened, fourier, precision=highest, preferred_element_type=jnp...  140 us
    psum x3, blocking collectives, paired_products(): lax.psum((jnp.sum(residual * adjusted), jnp.sum(applied * adjusted)), ('l...  130 us
    all_to_all x2, blocking collectives, precondition(): lax.all_to_all(coefficients, 'lat', split_axis=2, concat_axis=1, tiled=True)  22.9 us
    all_to_all x2, blocking collectives, meridional(): lax.all_to_all(returned, 'lat', split_axis=1, concat_axis=2, tiled=True)  19.5 us
    unnamed x12, local copies, waits for them, and re-layouts  13 us
    ppermute x3, waiting for transfers between devices, with_halo(): lax.ppermute(lax.slice_in_dim(block, 0, width, axis=dim), axis, backward)  12.7 us
  transfers between devices with their start and end apart: 8, of which 8 were waited for; matrix products, arithmetic and copies ran while one was open for 0% of the time, Pallas kernels for 0%

commit v1 on v0

v1 whole, which is shorter than its diff:
```python
import functools

import jax
import jax.numpy as jnp
import numpy as np
from jax import lax
from jax.experimental import pallas as pl
from jax.experimental.pallas import tpu as pltpu
from jax.sharding import PartitionSpec as P

WAVES = 640
ITERS = 3
RADIX = 16
LANES = 128
SHIFT = 1.0
MESH = pl.DeviceIdType.MESH
F32 = jnp.float32


class Plan:
    def __init__(self, mesh, levels, rows, longitudes):
        self.bands, self.columns = mesh.shape["lat"], mesh.shape["lev"]
        self.levels, self.rows, self.longitudes = levels, rows, longitudes
        self.latitudes = rows * self.bands
        assert longitudes == RADIX * LANES and rows % 8 == 0
        self.groups = max(1, self.bands // RADIX)
        self.per = max(1, RADIX // self.bands)
        assert self.bands * self.per == RADIX * self.groups
        high = WAVES // RADIX
        self.quota = high // self.groups
        assert self.quota * self.groups == high and 2 * self.quota <= LANES
        self.halo = -(-self.per * levels * 2 // 8) * 8
        self.own = self.per * levels * rows
        self.chunk = self.own + self.halo

    def tables(self):
        n, lat = self.longitudes, self.latitudes
        m1, i2 = np.arange(RADIX), np.arange(LANES)
        angle = 2 * np.pi * ((m1[:, None] * i2[None]) % n) / n
        twiddle = np.stack([np.cos(angle), np.sin(angle)])
        twiddle = np.broadcast_to(twiddle[:, :, None, :], (2, RADIX, 8, LANES))
        zonal = np.zeros((2 * LANES, self.groups * LANES))
        waves = np.zeros((self.bands * self.per, 1, LANES))
        for g in range(self.groups):
            m2 = g * self.quota + np.arange(self.quota)
            phi = 2 * np.pi * ((i2[:, None] * m2[None]) % LANES) / LANES
            block = np.block([[np.cos(phi), np.sin(phi)], [-np.sin(phi), np.cos(phi)]])
            zonal[:, g * LANES : g * LANES + 2 * self.quota] = block
            for low in range(RADIX):
                part = 4 * np.sin(np.pi * (low + RADIX * m2) / n) ** 2
                waves[low * self.groups + g, 0, : 2 * self.quota] = np.tile(part, 2)
        count = np.arange(1, lat + 1)
        sines = np.sin(np.pi * ((count[:, None] * count[None]) % (2 * lat + 2)) / (lat + 1))
        edges = np.zeros((self.bands, 2, lat))
        edges[1:, 0] = sines[self.rows - 1 : lat - 1 : self.rows]
        edges[:-1, 1] = sines[self.rows :: self.rows]
        returned = np.concatenate([sines, edges.reshape(-1, lat)])
        merid = 4 * np.sin(0.5 * np.pi * count / (lat + 1)) ** 2
        merid = np.broadcast_to(merid[:, None], (lat, LANES))
        theta = np.pi * (4 * np.arange(lat) + 3) / (4 * lat + 2)
        gain = 1 / np.maximum(np.sin(theta), 0.5) ** 2
        gain = np.broadcast_to(gain.reshape(self.bands, self.rows, 1), (self.bands, self.rows, LANES))
        found = (twiddle, zonal, zonal.T, waves, sines, returned, merid, gain)
        return [jnp.asarray(np.ascontiguousarray(t), F32) for t in found]


def combine(terms):
    total = None
    for factor, value in terms:
        if abs(factor) < 1e-12:
            continue
        term = value if abs(factor - 1) < 1e-12 else (-value if abs(factor + 1) < 1e-12 else F32(factor) * value)
        total = term if total is None else total + term
    return total


COS = np.cos(2 * np.pi * np.arange(16) / 16)
SIN = np.sin(2 * np.pi * np.arange(16) / 16)


def fold(v):
    e = {i: v[i] + v[16 - i] for i in range(1, 8)}
    o = {i: v[i] - v[16 - i] for i in range(1, 8)}
    e[0], e[8] = v[0], v[8]
    even = {i: e[i] + e[8 - i] for i in range(4)}
    odd = {i: e[i] - e[8 - i] for i in range(4)}
    even[4] = e[4]
    same = {i: o[i] + o[8 - i] for i in range(1, 4)}
    diff = {i: o[i] - o[8 - i] for i in range(1, 4)}
    same[4] = o[4]
    p, q = {}, {}
    for k in range(9):
        source = even if k % 2 == 0 else odd
        p[k] = combine([(COS[i * k % 16], x) for i, x in source.items()])
        if 0 < k < 8:
            source = diff if k % 2 == 0 else same
            q[k] = combine([(SIN[i * k % 16], x) for i, x in source.items()])
    return p, q


def unfold(p, q):
    even = {i: combine([(COS[i * k % 16], p[k]) for k in range(0, 9, 2)]) for i in range(5)}
    odd = {i: combine([(COS[i * k % 16], p[k]) for k in range(1, 9, 2)]) for i in range(4)}
    same = {i: combine([(SIN[i * k % 16], q[k]) for k in range(1, 8, 2)]) for i in range(1, 5)}
    diff = {i: combine([(SIN[i * k % 16], q[k]) for k in range(2, 8, 2)]) for i in range(1, 4)}
    e, o = {4: even[4]}, {4: same[4]}
    for i in range(4):
        e[i], e[8 - i] = even[i] + odd[i], even[i] - odd[i]
    for i in range(1, 4):
        o[i], o[8 - i] = same[i] + diff[i], same[i] - diff[i]
    v = {0: e[0], 8: e[8]}
    for i in range(1, 8):
        v[i], v[16 - i] = e[i] + o[i], e[i] - o[i]
    return [v[i] for i in range(16)]


def dot(a, b):
    return jnp.dot(a, b, precision=lax.Precision.HIGHEST, preferred_element_type=F32)


def kernel(
    plan,
    scale_ref, side_ref, shift_ref, twiddle, zonal, zonal_t, waves, sines, returned, merid, gain_ref,
    x_ref, r_ref,
    diag, half, basis, image, edge, spectrum, filtered, moments,
    send_f, recv_f, send_b, recv_b, send_h, recv_h, part_a, recv_a, part_c, recv_c,
    sf, rf, sb, rb, sh, rh, sa, ra, sc, rc,
):
    bands, columns, levels, rows = plan.bands, plan.columns, plan.levels, plan.rows
    per, groups, n = plan.per, plan.groups, plan.longitudes
    me, seat = lax.axis_index("lat"), lax.axis_index("lev")
    pending = []

    barrier = pltpu.get_barrier_semaphore()
    for off in range(1, bands):
        pl.semaphore_signal(
            barrier, inc=1, device_id={"lat": lax.rem(me + off, bands)}, device_id_type=MESH
        )
    for off in range(1, columns):
        pl.semaphore_signal(
            barrier, inc=1, device_id={"lev": lax.rem(seat + off, columns)}, device_id_type=MESH
        )

    def push(src, dst, send_sem, recv_sem, target):
        copy = pltpu.make_async_remote_copy(
            src_ref=src, dst_ref=dst, send_sem=send_sem, recv_sem=recv_sem,
            device_id=target, device_id_type=MESH,
        )
        copy.start()
        pending.append(copy)
        return copy

    gain = jnp.concatenate([gain_ref[me]] * RADIX, axis=1)
    scales = [scale_ref[k] for k in range(levels)]
    for k in range(levels):
        full = shift_ref[k] + scales[k] * (2.0 * gain + 2.5)
        diag[k] = full
        half[k] = 0.5 / full

    def analyse(source, it):
        for k in range(levels):
            whole = source[k]
            scaled = half[k] * whole
            send_h[it, 0, k] = scaled[:1]
            send_h[it, 1, k] = scaled[rows - 1 :]
            for row in range(0, rows, 8):
                p, q = fold([whole[row : row + 8, LANES * i : LANES * (i + 1)] for i in range(RADIX)])
                for low in range(RADIX):
                    c, s = twiddle[0, low], twiddle[1, low]
                    fp = p[min(low, RADIX - low)]
                    if low % 8 == 0:
                        zc, zs = fp * c, fp * s
                    else:
                        fq = q[low] if low < 8 else -q[RADIX - low]
                        zc, zs = fp * c - fq * s, fp * s + fq * c
                    start = (low * levels + k) * rows + row
                    spectrum[start : start + 8, :LANES] = zc
                    spectrum[start : start + 8, LANES:] = zs
        found = dot(spectrum[...], zonal[...])
        for low in range(RADIX):
            for g in range(groups):
                block = found[low * levels * rows : (low + 1) * levels * rows, g * LANES : (g + 1) * LANES]
                send_f[it, low * groups + g] = block

    def exchange(it):
        mine = pl.ds(me * per, per)
        copies = []
        for off in range(1, bands):
            target = lax.rem(me + off, bands)
            copies.append(push(
                send_f.at[it, pl.ds(target * per, per)], recv_f.at[it, mine],
                sf.at[it, off], rf.at[it, off], {"lat": target},
            ))
        edges = [
            push(send_h.at[it, 0], recv_h.at[it, 1], sh.at[it, 0], rh.at[it, 0],
                 {"lat": lax.rem(me + bands - 1, bands)}),
            push(send_h.at[it, 1], recv_h.at[it, 0], sh.at[it, 1], rh.at[it, 1],
                 {"lat": lax.rem(me + 1, bands)}),
        ]
        recv_f[it, mine] = send_f[it, mine]
        return copies, edges

    def meridional(it):
        blocks = []
        for p in range(per):
            for k in range(levels):
                blocks.append(jnp.concatenate(
                    [recv_f[it, s * per + p, k * rows : (k + 1) * rows, :] for s in range(bands)], axis=0
                ))
        modes = dot(sines[...], jnp.concatenate(blocks, axis=1)) * filtered[...]
        back = dot(returned[...], modes)
        lat = plan.latitudes
        for b in range(bands):
            for i in range(per * levels):
                lanes = slice(i * LANES, (i + 1) * LANES)
                send_b[it, b, i * rows : (i + 1) * rows, :] = back[b * rows : (b + 1) * rows, lanes]
                start = plan.own + 2 * i
                send_b[it, b, start : start + 2, :] = back[lat + 2 * b : lat + 2 * b + 2, lanes]
        copies = []
        for off in range(1, bands):
            target = lax.rem(me + off, bands)
            copies.append(push(
                send_b.at[it, target], recv_b.at[it, me], sb.at[it, off], rb.at[it, off], {"lat": target},
            ))
        recv_b[it, me] = send_b[it, me]
        return copies

    def synthesise(it, source):
        left = []
        for low in range(RADIX):
            blocks = []
            for g in range(groups):
                unit = low * groups + g
                start = unit % per * levels * rows
                blocks.append(recv_b[it, unit // per, start : start + levels * rows, :])
            left.append(jnp.concatenate(blocks, axis=1))
        for h in range(RADIX // per):
            left.append(jnp.concatenate(
                [recv_b[it, h * groups + g, plan.own :, :] for g in range(groups)], axis=1
            ))
        found = dot(jnp.concatenate(left, axis=0), zonal_t[...])
        base = RADIX * levels * rows

        def gather(block_of):
            p, q = {}, {}
            for low in range(RADIX):
                block = block_of(low)
                c, s = twiddle[0, low], twiddle[1, low]
                real, imag = block[:, :LANES], block[:, LANES:]
                index = min(low, RADIX - low)
                fp = real * c + imag * s
                p[index] = fp if index not in p else p[index] + fp
                if low % 8:
                    fq = imag * c - real * s
                    q[index] = fq if low < 8 else q[index] - fq
            return jnp.concatenate(unfold(p, q), axis=1)

        def beside(low):
            h, p = low // per, low % per
            block = found[base + h * plan.halo : base + h * plan.halo + plan.halo]
            block = block[p * 2 * levels : (p + 1) * 2 * levels]
            fill = 8 - 2 * levels
            return block if fill == 0 else jnp.concatenate([block, jnp.zeros((fill, 2 * LANES), F32)], axis=0)

        for k in range(levels):
            for row in range(0, rows, 8):
                field = gather(
                    lambda low: found[(low * levels + k) * rows + row : (low * levels + k) * rows + row + 8]
                )
                piece = slice(row, row + 8)
                field = field + half[k, piece] * source[k, piece]
                if it > 0:
                    field = field - SHIFT * basis[it - 1, k, piece]
                basis[it, k, piece] = field
        edge[it] = gather(beside)

    def apply(it):
        middle = n // 2
        for k in range(levels):
            field = basis[it, k]
            outer = []
            for side in range(2):
                r = 2 * k + side
                line = edge[it, r : r + 1] + recv_h[it, side, k]
                if it > 0:
                    line = line - SHIFT * edge[it - 1, r : r + 1]
                own = field[:1] if side == 0 else field[rows - 1 :]
                pole = jnp.concatenate([own[:, middle:], own[:, :middle]], axis=1)
                line = jnp.where(me == (0 if side == 0 else bands - 1), pole, line)
                edge[it, r : r + 1] = line
                outer.append(line)
            number = lax.broadcasted_iota(jnp.int32, (rows, n), 0)
            north = jnp.where(number == 0, outer[0], pltpu.roll(field, 1, 0))
            south = jnp.where(number == rows - 1, outer[1], pltpu.roll(field, rows - 1, 0))
            pair = north + south
            mixed = gain * field + 0.125 * pair
            coupling = pltpu.roll(mixed, 1, 1) + pltpu.roll(mixed, n - 1, 1) + pair
            image[it, k] = diag[k] * field - scales[k] * coupling

    def product(a, b):
        total = None
        for k in range(levels):
            value = a[k] * b[k]
            for i in range(RADIX):
                for row in range(0, rows, 8):
                    term = value[row : row + 8, LANES * i : LANES * (i + 1)]
                    total = term if total is None else total + term
        return jnp.sum(total, axis=0, keepdims=True)

    def moment(index):
        for i in range(index + 1):
            moments[index * (ITERS + 1) + i] = product(basis.at[i], image.at[index])
        moments[index * (ITERS + 1) + ITERS] = product(basis.at[index], side_ref)

    source = side_ref
    for it in range(ITERS):
        analyse(source, it)
        if it == 0:
            pl.semaphore_wait(barrier, bands - 1 + columns - 1)
        copies, edges = exchange(it)
        if it == 0:
            scaling = 2.0 / (n * (plan.latitudes + 1))
            for p in range(per):
                weight = scaling / (1.0 + merid[...] + waves[me * per + p])
                for k in range(levels):
                    place = p * levels + k
                    filtered[:, place * LANES : (place + 1) * LANES] = weight
        else:
            moment(it - 1)
        for copy in copies:
            copy.wait_recv()
        copies = meridional(it)
        for copy in copies + edges:
            copy.wait_recv()
        synthesise(it, source)
        apply(it)
        source = image.at[it]
    moment(ITERS - 1)

    lane = lax.broadcasted_iota(jnp.int32, (1, LANES), 1)
    places = [(i, j) for j in range(ITERS) for i in list(range(j + 1)) + [ITERS]]
    row = jnp.zeros((1, LANES), F32)
    for at, (i, j) in enumerate(places):
        value = jnp.sum(moments[j * (ITERS + 1) + i], axis=1, keepdims=True)
        row = row + jnp.where(lane == at, value, 0.0)

    def gather_sum(part, received, value, axis, here, count, send_sems, recv_sems):
        part[...] = value
        copies = []
        for off in range(1, count):
            copies.append(push(
                part, received.at[here], send_sems.at[off], recv_sems.at[off],
                {axis: lax.rem(here + off, count)},
            ))
        received[here] = value
        for copy in copies:
            copy.wait_recv()
        total = received[0]
        for i in range(1, count):
            total = total + received[i]
        return total

    row = gather_sum(part_a, recv_a, row, "lat", me, bands, sa, ra)
    row = gather_sum(part_c, recv_c, row, "lev", seat, columns, sc, rc)
    gram, load = {}, {}
    for at, (i, j) in enumerate(places):
        value = jnp.sum(jnp.where(lane == at, row, 0.0), axis=1, keepdims=True)
        if i == ITERS:
            load[j] = value
        else:
            gram[j, i] = value
    pivot, lower = {}, {}
    for j in range(ITERS):
        for i in range(j):
            for m in range(i):
                gram[j, i] = gram[j, i] - gram[j, m] * lower[i, m]
            lower[j, i] = gram[j, i] / pivot[i]
        pivot[j] = gram[j, j]
        for i in range(j):
            pivot[j] = pivot[j] - lower[j, i] * gram[j, i]
            load[j] = load[j] - lower[j, i] * load[i]
    weight = {}
    for j in reversed(range(ITERS)):
        weight[j] = load[j] / pivot[j]
        for i in range(j + 1, ITERS):
            weight[j] = weight[j] - lower[i, j] * weight[i]
    for k in range(levels):
        total, left = None, side_ref[k]
        for i in range(ITERS):
            term = weight[i] * basis[i, k]
            total = term if total is None else total + term
            left = left - weight[i] * image[i, k]
        x_ref[k] = total
        r_ref[k] = left
    for copy in pending:
        copy.wait_send()


def body(mesh, right_side, diag_shift, level_scale):
    levels, rows, n = right_side.shape
    plan = Plan(mesh, levels, rows, n)
    bands, columns, per = plan.bands, plan.columns, plan.per
    field = jax.ShapeDtypeStruct(right_side.shape, F32)
    vmem = pl.BlockSpec(memory_space=pltpu.VMEM)
    dma = pltpu.SemaphoreType.DMA
    units, block = bands * per, levels * rows
    tables = plan.tables()
    return pl.pallas_call(
        functools.partial(kernel, plan),
        out_shape=(field, field),
        in_specs=[pl.BlockSpec(memory_space=pltpu.SMEM)] + [vmem] * (2 + len(tables)),
        out_specs=(vmem, vmem),
        scratch_shapes=[
            pltpu.VMEM((levels, rows, n), F32),
            pltpu.VMEM((levels, rows, n), F32),
            pltpu.VMEM((ITERS, levels, rows, n), F32),
            pltpu.VMEM((ITERS, levels, rows, n), F32),
            pltpu.VMEM((ITERS, 8, n), F32),
            pltpu.VMEM((RADIX * block, 2 * LANES), F32),
            pltpu.VMEM((plan.latitudes, per * levels * LANES), F32),
            pltpu.VMEM((ITERS * (ITERS + 1), 1, LANES), F32),
            pltpu.VMEM((ITERS, units, block, LANES), F32),
            pltpu.VMEM((ITERS, units, block, LANES), F32),
            pltpu.VMEM((ITERS, bands, plan.chunk, LANES), F32),
            pltpu.VMEM((ITERS, bands, plan.chunk, LANES), F32),
            pltpu.VMEM((ITERS, 2, levels, 1, n), F32),
            pltpu.VMEM((ITERS, 2, levels, 1, n), F32),
            pltpu.VMEM((1, LANES), F32),
            pltpu.VMEM((bands, 1, LANES), F32),
            pltpu.VMEM((1, LANES), F32),
            pltpu.VMEM((columns, 1, LANES), F32),
            dma((ITERS, bands)), dma((ITERS, bands)), dma((ITERS, bands)), dma((ITERS, bands)),
            dma((ITERS, 2)), dma((ITERS, 2)),
            dma((bands,)), dma((bands,)), dma((columns,)), dma((columns,)),
        ],
        compiler_params=pltpu.CompilerParams(collective_id=0, has_side_effects=True),
    )(level_scale, right_side, diag_shift, *tables)


def solution(mesh):
    placed = (P("lev", "lat", None), P("lev", "lat", None), P("lev"))
    return jax.shard_map(
        functools.partial(body, mesh),
        mesh=mesh,
        in_specs=placed,
        out_specs=(P("lev", "lat", None), P("lev", "lat", None)),
        check_vma=False,
    )
```

time: 560 us -> 53.8 us (0.10); the launches traced: 551 us -> 53.7 us
  matrix products: 293 us -> 0 us
  blocking collectives: 172 us -> 0 us
  Pallas kernels: 0 us -> 50.8 us
  waiting for transfers between devices: 26.8 us -> 0 us
  starting transfers between devices: 21.1 us -> 0 us
  local copies, waits for them, and re-layouts: 20.1 us -> 2.26 us
  between operations: 11.2 us -> 0.65 us
  other arithmetic: 6.44 us -> 0 us
    dot_general x12 -> x0, matrix products: 293 us -> none  [the longest x3 150 us: precondition(): lax.dot_general(arrived.reshape(levels * band_rows, columns), fourier, ((...]
    psum x3 -> x0, blocking collectives: 130 us -> none  [paired_products(): lax.psum((jnp.sum(residual * adjusted), jnp.sum(applied * adjusted)), ('l...]
    pallas_call x0 -> x1, Pallas kernels: none -> 50.8 us  [body(): pl.pallas_call(functools.partial(kernel, plan), out_shape=(field, field),...]
    all_to_all x4 -> x0, blocking collectives: 42.3 us -> none  [the longest x2 22.9 us: precondition(): lax.all_to_all(coefficients, 'lat', split_axis=2, concat_axis=1, tiled=True)]
    all_to_all x2 -> x0, waiting for transfers between devices: 13.9 us -> none  [the longest x1 7.15 us: meridional(): lax.all_to_all(returned, 'lat', split_axis=1, concat_axis=2, tiled=True)]
    ppermute x6 -> x0, waiting for transfers between devices: 12.9 us -> none  [the longest x3 12.7 us: with_halo(): lax.ppermute(lax.slice_in_dim(block, 0, width, axis=dim), axis, backward)]
    all_to_all x2 -> x0, starting transfers between devices: 10.9 us -> none  [the longest x1 7.57 us: precondition(): lax.all_to_all(coefficients, 'lat', split_axis=2, concat_axis=1, tiled=True)]
    unnamed x12 -> x4, local copies, waits for them, and re-layouts: 13 us -> 2.26 us
  transfers between devices with their start and end apart: 8 -> 0, of which waited for: 8 -> 0; matrix products, arithmetic and copies ran while one was open for 0% -> 0% of each run, Pallas kernels for 0% -> 0%
where the time goes in v1:
time: 53.8 us; the launch traced here: 53.7 us
  Pallas kernels  50.8 us (94%)
  local copies, waits for them, and re-layouts  2.26 us (4%)
  between operations  0.65 us (1%)
    pallas_call x1, Pallas kernels, body(): pl.pallas_call(functools.partial(kernel, plan), out_shape=(field, field),...  50.8 us
    unnamed x4, local copies, waits for them, and re-layouts  2.26 us

profile of v1, /device:TPU:0, one launch (start us, length us, event | category | flops | bytes accessed | tf_op | source)
XLA Modules:
  0.0 53.7 jit_solution(8467775384547848112)
XLA Ops:
  0.6 50.8 %shard_map.122 = (f32[2,8,2048]{2,1,0:T(8,128)}, f32[2,8,2048]{2,1,0:T(8,128)}) custom-call(f32[2]{0:T(128)} %scale_ref.1, f32[2,8,2048]{2,1,0:T(8,128)} %side_ref.1, f32[2,8,2048]{2,1,0:T(8,128)} %shift_ref.1, f32[2,16,8,128]{3,2,1,0:T(8,128)} %constant.16.clone.twiddle, f32[256,128]{1,0:T(8,128)} %constant.17.clone.zonal, ...), custom_call_target="tpu_custom_call" | custom-call | tf_op jit(solution)/shard_map/pallas_call | solution.py:408
  51.4 0.0 copy-start
  51.4 1.6 %copy.15 = f32[2,8,2048]{2,1,0:T(8,128)} copy(f32[2,8,2048]{2,1,0:T(8,128)} %get-tuple-element.4) | data formatting | bytes 262144
  53.0 0.0 copy-done
  53.0 0.7 %copy.16 = f32[2,8,2048]{2,1,0:T(8,128)} copy(f32[2,8,2048]{2,1,0:T(8,128)S(1)} %copy-done) | data formatting | bytes 262144
Async XLA Ops:
  51.4 1.6 %copy-start = (f32[2,8,2048]{2,1,0:T(8,128)S(1)}, f32[2,8,2048]{2,1,0:T(8,128)}, u32[]{:S(2)}) copy-start(f32[2,8,2048]{2,1,0:T(8,128)} %get-tuple-element.5) | copy-start | bytes 393220

commit v2 on v1

--- a/solution.py
+++ b/solution.py
@@ -29,9 +29,14 @@
         high = WAVES // RADIX
         self.quota = high // self.groups
         assert self.quota * self.groups == high and 2 * self.quota <= LANES
-        self.halo = -(-self.per * levels * 2 // 8) * 8
-        self.own = self.per * levels * rows
-        self.chunk = self.own + self.halo
+        self.blocks = RADIX // self.per
+        self.span = 2 * self.per * self.quota
+        self.width = -(-self.span // LANES) * LANES
+        self.tiles = max(-(-levels * self.span // LANES), self.width // LANES)
+        self.lanes = self.tiles * LANES
+        assert levels <= 4
+        self.own = self.tiles * rows
+        self.chunk = self.own + -(-2 * self.tiles // 8) * 8
 
     def tables(self):
         n, lat = self.longitudes, self.latitudes
@@ -39,16 +44,20 @@
         angle = 2 * np.pi * ((m1[:, None] * i2[None]) % n) / n
         twiddle = np.stack([np.cos(angle), np.sin(angle)])
         twiddle = np.broadcast_to(twiddle[:, :, None, :], (2, RADIX, 8, LANES))
-        zonal = np.zeros((2 * LANES, self.groups * LANES))
-        waves = np.zeros((self.bands * self.per, 1, LANES))
+        zonal = np.zeros((self.per * 2 * LANES, self.groups * self.width))
+        waves = np.zeros((self.bands, 1, self.lanes))
         for g in range(self.groups):
             m2 = g * self.quota + np.arange(self.quota)
             phi = 2 * np.pi * ((i2[:, None] * m2[None]) % LANES) / LANES
             block = np.block([[np.cos(phi), np.sin(phi)], [-np.sin(phi), np.cos(phi)]])
-            zonal[:, g * LANES : g * LANES + 2 * self.quota] = block
-            for low in range(RADIX):
-                part = 4 * np.sin(np.pi * (low + RADIX * m2) / n) ** 2
-                waves[low * self.groups + g, 0, : 2 * self.quota] = np.tile(part, 2)
+            for p in range(self.per):
+                start = g * self.width + 2 * p * self.quota
+                zonal[2 * LANES * p : 2 * LANES * (p + 1), start : start + 2 * self.quota] = block
+                for h in range(self.blocks):
+                    part = 4 * np.sin(np.pi * (h * self.per + p + RADIX * m2) / n) ** 2
+                    for k in range(self.levels):
+                        start = k * self.span + 2 * p * self.quota
+                        waves[h * self.groups + g, 0, start : start + 2 * self.quota] = np.tile(part, 2)
         count = np.arange(1, lat + 1)
         sines = np.sin(np.pi * ((count[:, None] * count[None]) % (2 * lat + 2)) / (lat + 1))
         edges = np.zeros((self.bands, 2, lat))
@@ -56,7 +65,7 @@
         edges[:-1, 1] = sines[self.rows :: self.rows]
         returned = np.concatenate([sines, edges.reshape(-1, lat)])
         merid = 4 * np.sin(0.5 * np.pi * count / (lat + 1)) ** 2
-        merid = np.broadcast_to(merid[:, None], (lat, LANES))
+        merid = np.broadcast_to(merid[:, None], (lat, self.lanes))
         theta = np.pi * (4 * np.arange(lat) + 3) / (4 * lat + 2)
         gain = 1 / np.maximum(np.sin(theta), 0.5) ** 2
         gain = np.broadcast_to(gain.reshape(self.bands, self.rows, 1), (self.bands, self.rows, LANES))
@@ -122,9 +131,9 @@
     plan,
     scale_ref, side_ref, shift_ref, twiddle, zonal, zonal_t, waves, sines, returned, merid, gain_ref,
     x_ref, r_ref,
-    diag, half, basis, image, edge, spectrum, filtered, moments,
-    send_f, recv_f, send_b, recv_b, send_h, recv_h, part_a, recv_a, part_c, recv_c,
-    sf, rf, sb, rb, sh, rh, sa, ra, sc, rc,
+    diag, half, basis, image, edge, spectrum, lines, filtered, moments,
+    send_f, recv_f, send_b, recv_b, send_h, recv_h, part, parts,
+    sf, rf, sb, rb, sh, rh, sa, ra,
 ):
     bands, columns, levels, rows = plan.bands, plan.columns, plan.levels, plan.rows
     per, groups, n = plan.per, plan.groups, plan.longitudes
@@ -132,14 +141,13 @@
     pending = []
 
     barrier = pltpu.get_barrier_semaphore()
-    for off in range(1, bands):
-        pl.semaphore_signal(
-            barrier, inc=1, device_id={"lat": lax.rem(me + off, bands)}, device_id_type=MESH
-        )
-    for off in range(1, columns):
-        pl.semaphore_signal(
-            barrier, inc=1, device_id={"lev": lax.rem(seat + off, columns)}, device_id_type=MESH
-        )
+    for i in range(bands):
+        for j in range(columns):
+            if (i, j) != (0, 0):
+                pl.semaphore_signal(
+                    barrier, inc=1, device_id_type=MESH,
+                    device_id={"lat": lax.rem(me + i, bands), "lev": lax.rem(seat + j, columns)},
+                )
 
     def push(src, dst, send_sem, recv_sem, target):
         copy = pltpu.make_async_remote_copy(
@@ -156,6 +164,15 @@
         full = shift_ref[k] + scales[k] * (2.0 * gain + 2.5)
         diag[k] = full
         half[k] = 0.5 / full
+
+    def widen(block):
+        if plan.width == plan.lanes:
+            return block
+        return jnp.concatenate([block, jnp.zeros((rows, plan.lanes - plan.width), F32)], axis=1)
+
+    def turn(block, amount):
+        amount = amount % plan.lanes
+        return block if amount == 0 else pltpu.roll(block, amount, 1)
 
     def analyse(source, it):
         for k in range(levels):
@@ -173,73 +190,94 @@
                     else:
                         fq = q[low] if low < 8 else -q[RADIX - low]
                         zc, zs = fp * c - fq * s, fp * s + fq * c
-                    start = (low * levels + k) * rows + row
-                    spectrum[start : start + 8, :LANES] = zc
-                    spectrum[start : start + 8, LANES:] = zs
+                    start = (low // per * levels + k) * rows + row
+                    column = low % per * 2 * LANES
+                    spectrum[start : start + 8, column : column + LANES] = zc
+                    spectrum[start : start + 8, column + LANES : column + 2 * LANES] = zs
         found = dot(spectrum[...], zonal[...])
-        for low in range(RADIX):
+        for h in range(plan.blocks):
             for g in range(groups):
-                block = found[low * levels * rows : (low + 1) * levels * rows, g * LANES : (g + 1) * LANES]
-                send_f[it, low * groups + g] = block
+                total = None
+                for k in range(levels):
+                    start = (h * levels + k) * rows
+                    block = found[start : start + rows, g * plan.width : (g + 1) * plan.width]
+                    block = turn(widen(block), k * plan.span)
+                    total = block if total is None else total + block
+                send_f[it, h * groups + g] = total
+
+    def spread(source, received, it, send_sems, recv_sems):
+        copies = []
+        for i in range(bands - 1):
+            up = bands - 1 - i - (bands - 1 - i <= me).astype(jnp.int32)
+            down = i + (i >= me).astype(jnp.int32)
+            target = jnp.where(me < bands // 2, up, down)
+            copies.append(push(
+                source.at[it, target], received.at[it, me], send_sems.at[it, target], recv_sems.at[it, me],
+                {"lat": target},
+            ))
+        received[it, me] = source[it, me]
+        return [arrival(received, it, lax.rem(me + off, bands), recv_sems) for off in range(1, bands)]
+
+    def arrival(received, it, sender, recv_sems):
+        return pltpu.make_async_remote_copy(
+            src_ref=received.at[it, sender], dst_ref=received.at[it, sender],
+            send_sem=recv_sems.at[it, sender], recv_sem=recv_sems.at[it, sender],
+            device_id={"lat": sender}, device_id_type=MESH,
+        )
 
     def exchange(it):
-        mine = pl.ds(me * per, per)
-        copies = []
-        for off in range(1, bands):
-            target = lax.rem(me + off, bands)
-            copies.append(push(
-                send_f.at[it, pl.ds(target * per, per)], recv_f.at[it, mine],
-                sf.at[it, off], rf.at[it, off], {"lat": target},
-            ))
-        edges = [
-            push(send_h.at[it, 0], recv_h.at[it, 1], sh.at[it, 0], rh.at[it, 0],
-                 {"lat": lax.rem(me + bands - 1, bands)}),
-            push(send_h.at[it, 1], recv_h.at[it, 0], sh.at[it, 1], rh.at[it, 1],
-                 {"lat": lax.rem(me + 1, bands)}),
-        ]
-        recv_f[it, mine] = send_f[it, mine]
+        copies = spread(send_f, recv_f, it, sf, rf)
+        edges = []
+        for side, other in ((0, bands - 1), (1, 1)):
+            copy = pltpu.make_async_remote_copy(
+                src_ref=send_h.at[it, side], dst_ref=recv_h.at[it, 1 - side],
+                send_sem=sh.at[it, side], recv_sem=rh.at[it, side],
+                device_id={"lat": lax.rem(me + other, bands)}, device_id_type=MESH,
+            )
+            edges.append(copy)
+            pl.when(me != (bands - 1) * side)(copy.start)
         return copies, edges
 
     def meridional(it):
-        blocks = []
-        for p in range(per):
-            for k in range(levels):
-                blocks.append(jnp.concatenate(
-                    [recv_f[it, s * per + p, k * rows : (k + 1) * rows, :] for s in range(bands)], axis=0
-                ))
-        modes = dot(sines[...], jnp.concatenate(blocks, axis=1)) * filtered[...]
+        received = jnp.concatenate([recv_f[it, s] for s in range(bands)], axis=0)
+        modes = dot(sines[...], received) * filtered[...]
         back = dot(returned[...], modes)
         lat = plan.latitudes
         for b in range(bands):
-            for i in range(per * levels):
-                lanes = slice(i * LANES, (i + 1) * LANES)
-                send_b[it, b, i * rows : (i + 1) * rows, :] = back[b * rows : (b + 1) * rows, lanes]
-                start = plan.own + 2 * i
+            for t in range(plan.tiles):
+                lanes = slice(t * LANES, (t + 1) * LANES)
+                send_b[it, b, t * rows : (t + 1) * rows, :] = back[b * rows : (b + 1) * rows, lanes]
+                start = plan.own + 2 * t
                 send_b[it, b, start : start + 2, :] = back[lat + 2 * b : lat + 2 * b + 2, lanes]
-        copies = []
-        for off in range(1, bands):
-            target = lax.rem(me + off, bands)
-            copies.append(push(
-                send_b.at[it, target], recv_b.at[it, me], sb.at[it, off], rb.at[it, off], {"lat": target},
-            ))
-        recv_b[it, me] = send_b[it, me]
-        return copies
+        return spread(send_b, recv_b, it, sb, rb)
 
     def synthesise(it, source):
         left = []
-        for low in range(RADIX):
-            blocks = []
+        for h in range(plan.blocks):
+            for k in range(levels):
+                wide = []
+                for g in range(groups):
+                    parts = [recv_b[it, h * groups + g, t * rows : (t + 1) * rows, :] for t in range(plan.tiles)]
+                    wide.append(turn(jnp.concatenate(parts, axis=1), -k * plan.span)[:, : plan.width])
+                left.append(jnp.concatenate(wide, axis=1))
+        for h in range(plan.blocks):
             for g in range(groups):
-                unit = low * groups + g
-                start = unit % per * levels * rows
-                blocks.append(recv_b[it, unit // per, start : start + levels * rows, :])
-            left.append(jnp.concatenate(blocks, axis=1))
-        for h in range(RADIX // per):
-            left.append(jnp.concatenate(
-                [recv_b[it, h * groups + g, plan.own :, :] for g in range(groups)], axis=1
-            ))
+                for t in range(plan.tiles):
+                    start = g * plan.lanes + t * LANES
+                    pair = recv_b[it, h * groups + g, plan.own + 2 * t : plan.own + 2 * t + 2, :]
+                    for k in range(levels):
+                        lines[h, 2 * k : 2 * k + 2, start : start + LANES] = pair
+            level = lax.broadcasted_iota(jnp.int32, (8, plan.lanes), 0) // 2
+            wide = []
+            for g in range(groups):
+                both = lines[h, :, g * plan.lanes : (g + 1) * plan.lanes]
+                found = both
+                for k in range(1, levels):
+                    found = jnp.where(level == k, turn(both, -k * plan.span), found)
+                wide.append(found[:, : plan.width])
+            left.append(jnp.concatenate(wide, axis=1))
         found = dot(jnp.concatenate(left, axis=0), zonal_t[...])
-        base = RADIX * levels * rows
+        base = plan.blocks * levels * rows
 
         def gather(block_of):
             p, q = {}, {}
@@ -255,17 +293,17 @@
                     q[index] = fq if low < 8 else q[index] - fq
             return jnp.concatenate(unfold(p, q), axis=1)
 
+        def cut(start, low):
+            column = low % per * 2 * LANES
+            return found[start : start + 8, column : column + 2 * LANES]
+
         def beside(low):
-            h, p = low // per, low % per
-            block = found[base + h * plan.halo : base + h * plan.halo + plan.halo]
-            block = block[p * 2 * levels : (p + 1) * 2 * levels]
-            fill = 8 - 2 * levels
-            return block if fill == 0 else jnp.concatenate([block, jnp.zeros((fill, 2 * LANES), F32)], axis=0)
+            return cut(base + low // per * 8, low)
 
         for k in range(levels):
             for row in range(0, rows, 8):
                 field = gather(
-                    lambda low: found[(low * levels + k) * rows + row : (low * levels + k) * rows + row + 8]
+                    lambda low: cut((low // per * levels + k) * rows + row, low)
                 )
                 piece = slice(row, row + 8)
                 field = field + half[k, piece] * source[k, piece]
@@ -312,26 +350,25 @@
             moments[index * (ITERS + 1) + i] = product(basis.at[i], image.at[index])
         moments[index * (ITERS + 1) + ITERS] = product(basis.at[index], side_ref)
 
-    source = side_ref
+    source, beside = side_ref, []
     for it in range(ITERS):
         analyse(source, it)
         if it == 0:
-            pl.semaphore_wait(barrier, bands - 1 + columns - 1)
+            pl.semaphore_wait(barrier, bands * columns - 1)
         copies, edges = exchange(it)
         if it == 0:
             scaling = 2.0 / (n * (plan.latitudes + 1))
-            for p in range(per):
-                weight = scaling / (1.0 + merid[...] + waves[me * per + p])
-                for k in range(levels):
-                    place = p * levels + k
-                    filtered[:, place * LANES : (place + 1) * LANES] = weight
+            filtered[...] = scaling / (1.0 + merid[...] + waves[me])
         else:
             moment(it - 1)
         for copy in copies:
             copy.wait_recv()
         copies = meridional(it)
-        for copy in copies + edges:
+        for copy in copies:
             copy.wait_recv()
+        for side in range(2):
+            pl.when(me != (bands - 1) * (1 - side))(edges[side].wait_recv)
+            beside.append((side, edges[side]))
         synthesise(it, source)
         apply(it)
         source = image.at[it]
@@ -344,24 +381,20 @@
         value = jnp.sum(moments[j * (ITERS + 1) + i], axis=1, keepdims=True)
         row = row + jnp.where(lane == at, value, 0.0)
 
-    def gather_sum(part, received, value, axis, here, count, send_sems, recv_sems):
-        part[...] = value
-        copies = []
-        for off in range(1, count):
-            copies.append(push(
-                part, received.at[here], send_sems.at[off], recv_sems.at[off],
-                {axis: lax.rem(here + off, count)},
-            ))
-        received[here] = value
-        for copy in copies:
-            copy.wait_recv()
-        total = received[0]
-        for i in range(1, count):
-            total = total + received[i]
-        return total
-
-    row = gather_sum(part_a, recv_a, row, "lat", me, bands, sa, ra)
-    row = gather_sum(part_c, recv_c, row, "lev", seat, columns, sc, rc)
+    part[...] = row
+    arrivals = []
+    for i in range(bands - 1, -1, -1):
+        for j in range(columns):
+            if (i, j) != (0, 0):
+                copy = push(
+                    part, parts.at[me, seat], sa.at[i, j], ra.at[i, j],
+                    {"lat": lax.rem(me + i, bands), "lev": lax.rem(seat + j, columns)},
+                )
+                arrivals.append(copy)
+    parts[me, seat] = row
+    for copy in arrivals:
+        copy.wait_recv()
+    row = jnp.sum(parts[...].reshape(bands * columns, LANES), axis=0, keepdims=True)
     gram, load = {}, {}
     for at, (i, j) in enumerate(places):
         value = jnp.sum(jnp.where(lane == at, row, 0.0), axis=1, keepdims=True)
@@ -394,6 +427,8 @@
         r_ref[k] = left
     for copy in pending:
         copy.wait_send()
+    for side, copy in beside:
+        pl.when(me != (bands - 1) * side)(copy.wait_send)
 
 
 def body(mesh, right_side, diag_shift, level_scale):
@@ -403,7 +438,7 @@
     field = jax.ShapeDtypeStruct(right_side.shape, F32)
     vmem = pl.BlockSpec(memory_space=pltpu.VMEM)
     dma = pltpu.SemaphoreType.DMA
-    units, block = bands * per, levels * rows
+    block = levels * rows
     tables = plan.tables()
     return pl.pallas_call(
         functools.partial(kernel, plan),
@@ -416,22 +451,21 @@
             pltpu.VMEM((ITERS, levels, rows, n), F32),
             pltpu.VMEM((ITERS, levels, rows, n), F32),
             pltpu.VMEM((ITERS, 8, n), F32),
-            pltpu.VMEM((RADIX * block, 2 * LANES), F32),
-            pltpu.VMEM((plan.latitudes, per * levels * LANES), F32),
+            pltpu.VMEM((plan.blocks * block, per * 2 * LANES), F32),
+            pltpu.VMEM((plan.blocks, 8, plan.groups * plan.lanes), F32),
+            pltpu.VMEM((plan.latitudes, plan.lanes), F32),
             pltpu.VMEM((ITERS * (ITERS + 1), 1, LANES), F32),
-            pltpu.VMEM((ITERS, units, block, LANES), F32),
-            pltpu.VMEM((ITERS, units, block, LANES), F32),
+            pltpu.VMEM((ITERS, bands, rows, plan.lanes), F32),
+            pltpu.VMEM((ITERS, bands, rows, plan.lanes), F32),
             pltpu.VMEM((ITERS, bands, plan.chunk, LANES), F32),
             pltpu.VMEM((ITERS, bands, plan.chunk, LANES), F32),
             pltpu.VMEM((ITERS, 2, levels, 1, n), F32),
             pltpu.VMEM((ITERS, 2, levels, 1, n), F32),
             pltpu.VMEM((1, LANES), F32),
-            pltpu.VMEM((bands, 1, LANES), F32),
-            pltpu.VMEM((1, LANES), F32),
-            pltpu.VMEM((columns, 1, LANES), F32),
+            pltpu.VMEM((bands, columns, 1, LANES), F32),
             dma((ITERS, bands)), dma((ITERS, bands)), dma((ITERS, bands)), dma((ITERS, bands)),
             dma((ITERS, 2)), dma((ITERS, 2)),
-            dma((bands,)), dma((bands,)), dma((columns,)), dma((columns,)),
+            dma((bands, columns)), dma((bands, columns)),
         ],
         compiler_params=pltpu.CompilerParams(collective_id=0, has_side_effects=True),
     )(level_scale, right_side, diag_shift, *tables)

time: 53.8 us -> 49.5 us (0.920)
  Pallas kernels: 50.8 us -> 46.4 us
    pallas_call x1, Pallas kernels: 50.8 us -> 46.4 us  [body(): pl.pallas_call(functools.partial(kernel, plan), out_shape=(field, field),...]
where the time goes in v2:
time: 49.5 us; the launch traced here: 49.3 us
  Pallas kernels  46.4 us (94%)
  local copies, waits for them, and re-layouts  2.26 us (5%)
  between operations  0.65 us (1%)
    pallas_call x1, Pallas kernels, body(): pl.pallas_call(functools.partial(kernel, plan), out_shape=(field, field),...  46.4 us
    unnamed x4, local copies, waits for them, and re-layouts  2.26 us

profile of v2, /device:TPU:0, one launch (start us, length us, event | category | flops | bytes accessed | tf_op | source)
XLA Modules:
  0.0 49.3 jit_solution(12412214071557169568)
XLA Ops:
  0.6 46.4 %shard_map.122 = (f32[2,8,2048]{2,1,0:T(8,128)}, f32[2,8,2048]{2,1,0:T(8,128)}) custom-call(f32[2]{0:T(128)} %scale_ref.1, f32[2,8,2048]{2,1,0:T(8,128)} %side_ref.1, f32[2,8,2048]{2,1,0:T(8,128)} %shift_ref.1, f32[2,16,8,128]{3,2,1,0:T(8,128)} %constant.16.clone.twiddle, f32[512,256]{1,0:T(8,128)} %constant.17.clone.zonal, ...), custom_call_target="tpu_custom_call" | custom-call | tf_op jit(solution)/shard_map/pallas_call | solution.py:443
  47.0 0.0 copy-start
  47.1 1.6 %copy.15 = f32[2,8,2048]{2,1,0:T(8,128)} copy(f32[2,8,2048]{2,1,0:T(8,128)} %get-tuple-element.4) | data formatting | bytes 262144
  48.7 0.0 copy-done
  48.7 0.7 %copy.16 = f32[2,8,2048]{2,1,0:T(8,128)} copy(f32[2,8,2048]{2,1,0:T(8,128)S(1)} %copy-done) | data formatting | bytes 262144
Async XLA Ops:
  47.0 1.6 %copy-start = (f32[2,8,2048]{2,1,0:T(8,128)S(1)}, f32[2,8,2048]{2,1,0:T(8,128)}, u32[]{:S(2)}) copy-start(f32[2,8,2048]{2,1,0:T(8,128)} %get-tuple-element.5) | copy-start | bytes 393220

commit v3 on v2

--- a/solution.py
+++ b/solution.py
@@ -130,7 +130,7 @@
 def kernel(
     plan,
     scale_ref, side_ref, shift_ref, twiddle, zonal, zonal_t, waves, sines, returned, merid, gain_ref,
-    x_ref, r_ref,
+    out_ref,
     diag, half, basis, image, edge, spectrum, lines, filtered, moments,
     send_f, recv_f, send_b, recv_b, send_h, recv_h, part, parts,
     sf, rf, sb, rb, sh, rh, sa, ra,
@@ -251,7 +251,7 @@
                 send_b[it, b, start : start + 2, :] = back[lat + 2 * b : lat + 2 * b + 2, lanes]
         return spread(send_b, recv_b, it, sb, rb)
 
-    def synthesise(it, source):
+    def synthesise(it):
         left = []
         for h in range(plan.blocks):
             for k in range(levels):
@@ -306,10 +306,7 @@
                     lambda low: cut((low // per * levels + k) * rows + row, low)
                 )
                 piece = slice(row, row + 8)
-                field = field + half[k, piece] * source[k, piece]
-                if it > 0:
-                    field = field - SHIFT * basis[it - 1, k, piece]
-                basis[it, k, piece] = field
+                basis[it, k, piece] = field + basis[it, k, piece]
         edge[it] = gather(beside)
 
     def apply(it):
@@ -364,12 +361,15 @@
         for copy in copies:
             copy.wait_recv()
         copies = meridional(it)
+        for k in range(levels):
+            known = half[k] * source[k]
+            basis[it, k] = known - SHIFT * basis[it - 1, k] if it > 0 else known
         for copy in copies:
             copy.wait_recv()
         for side in range(2):
             pl.when(me != (bands - 1) * (1 - side))(edges[side].wait_recv)
             beside.append((side, edges[side]))
-        synthesise(it, source)
+        synthesise(it)
         apply(it)
         source = image.at[it]
     moment(ITERS - 1)
@@ -423,8 +423,8 @@
             term = weight[i] * basis[i, k]
             total = term if total is None else total + term
             left = left - weight[i] * image[i, k]
-        x_ref[k] = total
-        r_ref[k] = left
+        out_ref[0, k] = total
+        out_ref[1, k] = left
     for copy in pending:
         copy.wait_send()
     for side, copy in beside:
@@ -435,16 +435,16 @@
     levels, rows, n = right_side.shape
     plan = Plan(mesh, levels, rows, n)
     bands, columns, per = plan.bands, plan.columns, plan.per
-    field = jax.ShapeDtypeStruct(right_side.shape, F32)
+    field = jax.ShapeDtypeStruct((2, *right_side.shape), F32)
     vmem = pl.BlockSpec(memory_space=pltpu.VMEM)
     dma = pltpu.SemaphoreType.DMA
     block = levels * rows
     tables = plan.tables()
-    return pl.pallas_call(
+    both = pl.pallas_call(
         functools.partial(kernel, plan),
-        out_shape=(field, field),
+        out_shape=field,
         in_specs=[pl.BlockSpec(memory_space=pltpu.SMEM)] + [vmem] * (2 + len(tables)),
-        out_specs=(vmem, vmem),
+        out_specs=vmem,
         scratch_shapes=[
             pltpu.VMEM((levels, rows, n), F32),
             pltpu.VMEM((levels, rows, n), F32),
@@ -469,6 +469,7 @@
         ],
         compiler_params=pltpu.CompilerParams(collective_id=0, has_side_effects=True),
     )(level_scale, right_side, diag_shift, *tables)
+    return both[0], both[1]
 
 
 def solution(mesh):

time: 49.5 us -> 48.9 us (0.988)
  local copies, waits for them, and re-layouts: 2.26 us -> 1.69 us
    unnamed x4 -> x0, local copies, waits for them, and re-layouts: 2.26 us -> none
    squeeze x0 -> x1, local copies, waits for them, and re-layouts: none -> 1.69 us  [body(): return (both[0], both[1])]
where the time goes in v3:
time: 48.9 us; the launch traced here: 48.7 us
  Pallas kernels  46.4 us (95%)
  local copies, waits for them, and re-layouts  1.69 us (3%)
  between operations  0.64 us (1%)
    pallas_call x1, Pallas kernels, body(): pl.pallas_call(functools.partial(kernel, plan), out_shape=field, in_specs...  46.4 us
    squeeze x1, local copies, waits for them, and re-layouts, body(): return (both[0], both[1])  1.69 us

profile of v3, /device:TPU:0, one launch (start us, length us, event | category | flops | bytes accessed | tf_op | source)
XLA Modules:
  0.0 48.7 jit_solution(12731627718922811896)
XLA Ops:
  0.6 46.4 %shard_map.122 = f32[2,2,8,2048]{3,2,1,0:T(8,128)} custom-call(f32[2]{0:T(128)} %scale_ref.1, f32[2,8,2048]{2,1,0:T(8,128)} %side_ref.1, f32[2,8,2048]{2,1,0:T(8,128)} %shift_ref.1, f32[2,16,8,128]{3,2,1,0:T(8,128)} %constant.16.clone.twiddle, f32[512,256]{1,0:T(8,128)} %constant.17.clone.zonal, f32[256,512]{1,0:T(8,128)} %constant.18.clone.zonal_t, ...), custom_call_target="tpu_custom_call" | custom-call | tf_op jit(solution)/shard_map/pallas_call | solution.py:443
  47.1 1.7 %slice_bitcast_fusion = (f32[2,8,2048]{2,1,0:T(8,128)}, f32[2,8,2048]{2,1,0:T(8,128)}) fusion(f32[2,2,8,2048]{3,2,1,0:T(8,128)} %shard_map.122), kind=kLoop, calls=%fused_computation | loop fusion | bytes 524288 | tf_op jit(solution)/shard_map/squeeze | solution.py:472
